TPU v7x, 128 devices: a whole 4x4x4 slice. The times are simulated.
128 devices in a mesh: level: 4 (over x_lo, core), space: 32 (over y, x_hi, z).
Axes of the slice: x: 4 (x_hi: 2, x_lo: 2; x = x_hi * 2 + x_lo), y: 4, z: 4, core: 2. Of those that a mesh axis runs over, the one named last changes fastest.
Arguments:
- u_init: float32 [1024, 2048], P('space'), may hold values from 0.2 to 1
- v_init: float32 [1024, 2048], P('space'), may hold values from 0 to 0.5
- feed_rate: float32 [1024, 2048], P('space'), may hold values from 0.01 to 0.12
- kill_rate: float32 [1024, 2048], P('space'), may hold values from 0.02 to 0.16
Outputs:
- level_states: float32 [4, 2, 1024, 2048], P('level', None, 'space')
All inputs are finite; a program needn't handle non-finite values.
Results may differ from a plain program's by a relative error of at most 0.0003.
Values sent between devices are 32-bit elements; how exact they have to be, the bound alone decides.
A program may use at most 64 MiB of HBM per device.

v0:
```python
import jax
import jax.numpy as jnp
from jax import lax
from jax.experimental import pallas as pl
from jax.experimental.pallas import tpu as pltpu
from jax.sharding import PartitionSpec as P

STEPS = 4
LEVELS = 4
LANES = 128
TILES = 4
RING = TILES + 1
OFF = 56
MESH = pl.DeviceIdType.MESH

SOURCE_RADIUS = [[42, 39, 36, 15], [32, 29, 26, 11], [22, 19, 16, 7], [12, 9, 6, 3]]


def span(own, radius):
    low = (OFF - radius) // 8 * 8
    high = -(-(OFF + own + radius) // 8) * 8
    return low, high


def over_rows(low, high, chunk, body):
    count = (high - low) // chunk

    def step(i, carry):
        body(low + i * chunk, chunk)
        return carry

    if count:
        lax.fori_loop(0, count, step, 0, unroll=True)
    if low + count * chunk < high:
        body(low + count * chunk, high - low - count * chunk)


def around(ref, row, rows):
    mid = ref[:, pl.ds(row, rows), :]
    lane = lax.broadcasted_iota(jnp.int32, (1, rows, LANES), 2)
    to_right = pltpu.roll(mid, 1, 2)
    to_left = pltpu.roll(mid, LANES - 1, 2)
    left = jnp.where(lane == 0, jnp.concatenate([to_right[-1:], to_right[:-1]], 0), to_right)
    right = jnp.where(
        lane == LANES - 1, jnp.concatenate([to_left[1:], to_left[:1]], 0), to_left
    )
    return mid, (left + right) + (ref[:, pl.ds(row - 1, rows), :] + ref[:, pl.ds(row + 1, rows), :])


def kernel(own, u_hbm, v_hbm, f_hbm, k_hbm, out, inp, side, node, force, first, work, fin,
           load_sem, side_sem, send_sem, recv_sem, put_sem, got_sem):
    level = lax.axis_index("level")
    space = lax.axis_index("space")
    blocks = lax.axis_size("space")
    cols = TILES * LANES
    near = [lax.rem(space + step, blocks) for step in (1, 2, blocks - 1, blocks - 2)]

    barrier = pltpu.get_barrier_semaphore()
    for peer in near:
        pl.semaphore_signal(barrier, inc=1, device_id={"space": peer}, device_id_type=MESH)
    for step in range(1, LEVELS):
        pl.semaphore_signal(
            barrier, inc=1, device_id={"level": lax.rem(level + step, LEVELS)}, device_id_type=MESH
        )

    left_col = pl.multiple_of(lax.rem(level + LEVELS - 1, LEVELS) * cols + cols - LANES, LANES)
    right_col = pl.multiple_of(lax.rem(level + 1, LEVELS) * cols, LANES)
    home = pl.ds(OFF, own)
    loads = []
    sides = []
    for at, field in enumerate((u_hbm, v_hbm, f_hbm, k_hbm)):
        for tile in range(TILES):
            col = pl.multiple_of(level * cols + tile * LANES, LANES)
            loads.append(pltpu.make_async_copy(
                field.at[:, pl.ds(col, LANES)], inp.at[at, tile, home, :], load_sem.at[at, tile]))
        for end, col in enumerate((left_col, right_col)):
            sides.append(pltpu.make_async_copy(
                field.at[:, pl.ds(col, LANES)], side.at[at, end], side_sem.at[at, end]))
    for copy in loads + sides:
        copy.start()
    for copy in sides:
        copy.wait()
    half = lax.broadcasted_iota(jnp.int32, (4, own, LANES), 2) < LANES // 2
    inp[:, TILES, home, :] = jnp.where(half, side[:, 1], side[:, 0])
    for copy in loads:
        copy.wait()
    pl.semaphore_wait(barrier, len(near) + LEVELS - 1)

    moves = [
        (OFF, OFF - own, own, near[0]),
        (OFF, OFF + own, own, near[2]),
        (OFF + own - 16, OFF - own - 16, 16, near[1]),
        (OFF, OFF + 2 * own, 16, near[3]),
    ]
    sends = []
    for part, tiles in enumerate((pl.ds(0, TILES), pl.ds(TILES, 1))):
        for at, (row, row_there, rows, peer) in enumerate(moves):
            sends.append(pltpu.make_async_remote_copy(
                inp.at[:, tiles, pl.ds(row, rows), :],
                inp.at[:, tiles, pl.ds(row_there, rows), :],
                send_sem.at[part, at], recv_sem.at[part, at],
                device_id={"space": peer}, device_id_type=MESH))
    for copy in sends:
        copy.start()
    for copy in sends:
        copy.wait()

    def rates(row, rows):
        here = pl.ds(row, rows)
        feed = inp[2, :, here, :]
        return feed, feed + inp[3, :, here, :]

    def react(u, v, feed, both):
        cubic = u * v * v
        return feed * (1.0 - u) - cubic, cubic - both * v

    def lap_of(ref, row, rows):
        mid, near_sum = around(ref, row, rows)
        return mid, near_sum - 4.0 * mid

    def first_forcing(row, rows):
        here = pl.ds(row, rows)
        feed, both = rates(row, rows)
        u, lap_u = lap_of(inp.at[0], row, rows)
        v, lap_v = lap_of(inp.at[1], row, rows)
        rea = react(u, v, feed, both)
        for field, total in enumerate((lap_u + rea[0], 0.5 * lap_v + rea[1])):
            first[0, field, :, here, :] = (9.0 / 24.0) * total - rea[field]
            first[1, field, :, here, :] = (1.0 / 24.0) * total

    def forcing(last, row, rows):
        here = pl.ds(row, rows)
        feed, both = rates(row, rows)
        count = STEPS if last else STEPS - 1
        laps = []
        reas = []
        for at in range(count):
            u, lap_u = lap_of(node.at[at, 0], row, rows)
            v, lap_v = lap_of(node.at[at, 1], row, rows)
            laps.append((lap_u, 0.5 * lap_v))
            if at < STEPS - 1 or last:
                reas.append(react(u, v, feed, both))
        for field in range(2):
            lap = [None] + [value[field] for value in laps]
            rea = [None] + [value[field] for value in reas]
            full = [None] + [a + b for a, b in zip(lap[1:], rea[1:])]
            nine = first[0, field, :, here, :]
            one = first[1, field, :, here, :]
            third = (1.0 / 24.0) * full[3]
            second = (5.0 / 24.0) * full[2]
            force[0, field, :, here, :] = (nine - lap[1]) + (19.0 / 24.0) * full[1] - second + third
            force[1, field, :, here, :] = (
                (13.0 / 24.0) * (full[1] + full[2]) - (one + third) - (lap[2] + rea[1]))
            force[2, field, :, here, :] = (
                (one - (lap[3] + rea[2])) - (5.0 / 24.0) * full[1]
                + (19.0 / 24.0) * full[2] + (9.0 / 24.0) * full[3])
            if last:
                force[3, field, :, here, :] = (
                    (1.0 / 24.0) * full[1] - second + (19.0 / 24.0) * full[3]
                    + (9.0 / 24.0) * full[4] - (lap[4] + rea[3]))

    def source(level_num, step_num, u_ref, v_ref, row, rows):
        here = pl.ds(row, rows)
        feed, both = rates(row, rows)
        u = u_ref[:, here, :]
        v = v_ref[:, here, :]
        rea_u, rea_v = react(u, v, feed, both)
        u = u + rea_u
        v = v + rea_v
        if level_num:
            u = u + force[step_num, 0, :, here, :]
            v = v + force[step_num, 1, :, here, :]
        work[0, 0, :, here, :] = 0.2 * u
        work[0, 1, :, here, :] = (1.0 / 3.0) * v

    def sweep(old, new, scale, field, row, rows):
        here = pl.ds(row, rows)
        _, near_sum = around(old, row, rows)
        if scale != 1.0:
            near_sum = scale * near_sum
        new[:, here, :] = work[0, field, :, here, :] + near_sum

    def last_sweep(old, scale, dest, field, row, rows):
        _, near_sum = around(old, row, rows)
        value = work[0, field, :, pl.ds(row, rows), :] + scale * near_sum
        for tile in range(TILES):
            dest[field, pl.ds(row - OFF, rows), pl.ds(tile * LANES, LANES)] = value[tile]

    puts = []
    for level_num in range(LEVELS):
        radii = SOURCE_RADIUS[level_num]
        if level_num == 1:
            over_rows(*span(own, radii[0]), 8, first_forcing)
        if level_num:
            low, high = span(own, radii[0])
            low_in, high_in = span(own, radii[3])
            over_rows(low, low_in, 8, lambda row, rows: forcing(False, row, rows))
            over_rows(low_in, high_in, 8, lambda row, rows: forcing(True, row, rows))
            over_rows(high_in, high, 8, lambda row, rows: forcing(False, row, rows))
        for step_num in range(STEPS):
            refs = [inp.at[field] if step_num == 0 else node.at[step_num - 1, field] for field in range(2)]
            radius = radii[step_num]
            over_rows(*span(own, radius), 16,
                      lambda row, rows: source(level_num, step_num, refs[0], refs[1], row, rows))
            for sweep_num in range(3):
                extent = span(own, radius - sweep_num - 1)
                for field, scale in enumerate((0.2, 1.0 / 6.0)):
                    old = work.at[sweep_num, field]
                    new = node.at[step_num, field] if sweep_num == 2 else work.at[sweep_num + 1, field]
                    factor = scale if sweep_num else (1.0, 0.5)[field]
                    if level_num == LEVELS - 1 and step_num == STEPS - 1 and sweep_num == 2:
                        over_rows(OFF, OFF + own, 16, lambda row, rows: last_sweep(
                            old, factor, fin.at[level_num], field, row, rows))
                    else:
                        over_rows(*extent, 16, lambda row, rows: sweep(
                            old, new, factor, field, row, rows))
        if level_num < LEVELS - 1:
            for field in range(2):
                for tile in range(TILES):
                    fin[level_num, field, :, pl.ds(tile * LANES, LANES)] = (
                        node[STEPS - 1, field, tile, home, :])
        place = out.at[0, :, :, pl.ds(pl.multiple_of(level * cols, LANES), cols)]
        mine = pltpu.make_async_copy(fin.at[level_num], place, put_sem.at[level_num])
        theirs = pltpu.make_async_remote_copy(
            fin.at[level_num], place, put_sem.at[level_num], got_sem.at[level],
            device_id={"level": level_num}, device_id_type=MESH)
        puts.append((mine, theirs))

        @pl.when(level == level_num)
        def _():
            mine.start()

        @pl.when(level != level_num)
        def _():
            theirs.start()

    for level_num, (mine, theirs) in enumerate(puts):
        @pl.when(level == level_num)
        def _():
            mine.wait()

        @pl.when(level != level_num)
        def _():
            theirs.wait_send()

    for step in range(1, LEVELS):
        source_level = lax.rem(level + step, LEVELS)
        place = out.at[0, :, :, pl.ds(pl.multiple_of(source_level * cols, LANES), cols)]
        pltpu.make_async_remote_copy(
            fin.at[0], place, put_sem.at[0], got_sem.at[source_level],
            device_id={"level": source_level}, device_id_type=MESH).wait_recv()


def body(u_init, v_init, feed_rate, kill_rate):
    own, width = u_init.shape
    rows = OFF + own + 56
    field = (RING, rows, LANES)
    anywhere = pl.BlockSpec(memory_space=pl.ANY)
    dma = pltpu.SemaphoreType.DMA
    return pl.pallas_call(
        lambda *refs: kernel(own, *refs),
        out_shape=jax.ShapeDtypeStruct((1, 2, own, width), jnp.float32),
        in_specs=[anywhere] * 4,
        out_specs=anywhere,
        scratch_shapes=[
            pltpu.VMEM((4,) + field, jnp.float32),
            pltpu.VMEM((4, 2, own, LANES), jnp.float32),
            pltpu.VMEM((STEPS, 2) + field, jnp.float32),
            pltpu.VMEM((STEPS, 2) + field, jnp.float32),
            pltpu.VMEM((2, 2) + field, jnp.float32),
            pltpu.VMEM((3, 2) + field, jnp.float32),
            pltpu.VMEM((LEVELS, 2, own, TILES * LANES), jnp.float32),
            dma((4, TILES)), dma((4, 2)), dma((2, 4)), dma((2, 4)), dma((LEVELS,)), dma((LEVELS,)),
        ],
        compiler_params=pltpu.CompilerParams(
            collective_id=0, has_side_effects=True, vmem_limit_bytes=48 * 1024 * 1024),
        name="window",
    )(u_init, v_init, feed_rate, kill_rate)


def solution(mesh):
    return jax.shard_map(
        body,
        mesh=mesh,
        in_specs=(P("space", None),) * 4,
        out_specs=P("level", None, "space", None),
        check_vma=False,
    )
```

profile of v0, /device:TPU:3, one launch (start us, length us, event | category | flops | bytes accessed | tf_op | source)
XLA Modules:
  0.0 47.7 jit_solution(14845517531462098163)
XLA Ops:
  0.0 0.0 copy-start
  0.0 0.9 %copy-done = f32[32,2048]{1,0:T(8,128)S(1)} copy-done((f32[32,2048]{1,0:T(8,128)S(1)}, f32[32,2048]{1,0:T(8,128)}, u32[]{:S(2)}) %copy-start) | copy-done | bytes 262168
  1.0 0.0 copy-start.1
  1.0 0.9 %copy-done.1 = f32[32,2048]{1,0:T(8,128)S(1)} copy-done((f32[32,2048]{1,0:T(8,128)S(1)}, f32[32,2048]{1,0:T(8,128)}, u32[]{:S(2)}) %copy-start.1) | copy-done | bytes 262168
  1.9 0.0 copy-start.2
  1.9 0.9 %copy-done.2 = f32[32,2048]{1,0:T(8,128)S(1)} copy-done((f32[32,2048]{1,0:T(8,128)S(1)}, f32[32,2048]{1,0:T(8,128)}, u32[]{:S(2)}) %copy-start.2) | copy-done | bytes 262168
  2.9 0.0 copy-start.3
  2.9 0.9 %copy-done.3 = f32[32,2048]{1,0:T(8,128)S(1)} copy-done((f32[32,2048]{1,0:T(8,128)S(1)}, f32[32,2048]{1,0:T(8,128)}, u32[]{:S(2)}) %copy-start.3) | copy-done | bytes 262168
  3.8 43.1 %window.1 = f32[1,2,32,2048]{3,2,1,0:T(8,128)S(1)} custom-call(f32[32,2048]{1,0:T(8,128)S(1)} %copy-done, f32[32,2048]{1,0:T(8,128)S(1)} %copy-done.1, f32[32,2048]{1,0:T(8,128)S(1)} %copy-done.2, f32[32,2048]{1,0:T(8,128)S(1)} %copy-done.3), custom_call_target="tpu_custom_call" | custom-call | tf_op jit(solution)/shard_map/window/pallas_call | solution.py:260
  46.9 0.8 %copy.6 = f32[1,2,32,2048]{3,2,1,0:T(8,128)} copy(f32[1,2,32,2048]{3,2,1,0:T(8,128)S(1)} %window.1) | data formatting | bytes 1048576
Async XLA Ops:
  0.0 0.9 %copy-start = (f32[32,2048]{1,0:T(8,128)S(1)}, f32[32,2048]{1,0:T(8,128)}, u32[]{:S(2)}) copy-start(f32[32,2048]{1,0:T(8,128)} %refs_0_.1) | copy-start | bytes 786436
  1.0 0.9 %copy-start.1 = (f32[32,2048]{1,0:T(8,128)S(1)}, f32[32,2048]{1,0:T(8,128)}, u32[]{:S(2)}) copy-start(f32[32,2048]{1,0:T(8,128)} %refs_1_.1) | copy-start | bytes 786436
  1.9 0.9 %copy-start.2 = (f32[32,2048]{1,0:T(8,128)S(1)}, f32[32,2048]{1,0:T(8,128)}, u32[]{:S(2)}) copy-start(f32[32,2048]{1,0:T(8,128)} %refs_2_.1) | copy-start | bytes 786436
  2.9 0.9 %copy-start.3 = (f32[32,2048]{1,0:T(8,128)S(1)}, f32[32,2048]{1,0:T(8,128)}, u32[]{:S(2)}) copy-start(f32[32,2048]{1,0:T(8,128)} %refs_3_.1) | copy-start | bytes 786436
where the time goes:
time: 48 us; the launch traced here: 47.7 us
  Pallas kernels  43.1 us (90%)
  local copies, waits for them, and re-layouts  4.59 us (10%)
    pallas_call x1, Pallas kernels, body(): pl.pallas_call(lambda *refs: kernel(own, *refs), out_shape=jax.ShapeDtype...  43.1 us
    unnamed x9, local copies, waits for them, and re-layouts  4.59 us

commit v1 on v0

v1 whole, which is shorter than its diff:
```python
import jax
import jax.numpy as jnp
from jax import lax
from jax.experimental import pallas as pl
from jax.experimental.pallas import tpu as pltpu
from jax.sharding import PartitionSpec as P

STEPS = 4
LEVELS = 4
LANES = 128
TILES = 4
RING = TILES + 1
OFF = 48
REACH = 42
CHUNK = 16
RUN = 4
MESH = pl.DeviceIdType.MESH

FULL = [[42, 39, 36, 15], [32, 29, 26, 11], [22, 19, 16, 7], [12, 9, 6, 3]]
KNOWN = [[10 * level + 3 * step + 6 for step in range(STEPS)] for level in range(LEVELS)]


def room(radius):
    at = (radius + 16) // 8 * 8
    return at, (at + 32 + radius + 16) // 8 * 8


class Field:
    def __init__(self, ref, at):
        self.ref, self.at = ref, at

    def load(self, field, row, rows):
        return self.ref[field, :, pl.ds(row + self.at, rows), :]

    def store(self, field, row, rows, value):
        self.ref[field, :, pl.ds(row + self.at, rows), :] = value

    def around(self, field, row, rows):
        mid = self.load(field, row, rows)
        left = jnp.concatenate([pltpu.roll(mid[RING - 1:], 1, 2), mid[:RING - 1]], 0)
        right = jnp.concatenate([mid[1:], pltpu.roll(mid[:1], LANES - 1, 2)], 0)
        vertical = self.load(field, row - 1, rows) + self.load(field, row + 1, rows)
        return mid, (left + right) + vertical


def over_rows(spans, chunk, body):
    for low, high, upward in spans:
        count = (high - low + 7) // 8 * 8
        if count <= 0:
            continue
        low = high - count if upward else low
        rest = count % chunk
        if rest:
            body(low, rest)

        def step(i, carry, low=low + rest):
            body(low + i * chunk, chunk)
            return carry

        if count // chunk:
            lax.fori_loop(0, count // chunk, step, 0, unroll=True)


def kernel(own, u_hbm, v_hbm, f_hbm, k_hbm, out, inp, nat, turn, fin, turn_out, *rest):
    fields, (load_sem, send_sem, recv_sem, put_sem, got_sem, ready) = list(rest[:-6]), rest[-6:]
    level = lax.axis_index("level")
    space = lax.axis_index("space")
    blocks = lax.axis_size("space")
    cols = TILES * LANES
    after, before = lax.rem(space + 1, blocks), lax.rem(space + blocks - 1, blocks)

    barrier = pltpu.get_barrier_semaphore()
    pl.semaphore_signal(barrier, inc=1, device_id={"space": before}, device_id_type=MESH)
    for step in range(1, LEVELS):
        pl.semaphore_signal(
            barrier, inc=1, device_id={"level": lax.rem(level + step, LEVELS)}, device_id_type=MESH
        )

    starts = [level * cols + tile * LANES for tile in range(TILES)]
    starts.append(lax.rem(level + LEVELS - 1, LEVELS) * cols + cols - LANES)
    starts.append(lax.rem(level + 1, LEVELS) * cols)
    loads = []
    for tile, col in enumerate(starts):
        for at, field in enumerate((u_hbm, v_hbm, f_hbm, k_hbm)):
            loads.append(pltpu.make_async_copy(
                field.at[:, pl.ds(pl.multiple_of(col, LANES), LANES)],
                nat.at[tile, pl.ds(at * own, own), :], load_sem.at[tile, at]))
    for copy in loads:
        copy.start()
    pl.semaphore_wait(barrier, LEVELS)
    pl.semaphore_signal(ready, inc=1, device_id={"space": after}, device_id_type=MESH)
    for copy in loads:
        copy.wait()
    half = lax.broadcasted_iota(jnp.int32, (4 * own, LANES), 1) < LANES // 2
    for tile in range(RING):
        value = nat[tile] if tile < TILES else jnp.where(half, nat[TILES + 1], nat[TILES])
        turn[pl.ds(tile * LANES, LANES), :] = value.T
    for strip in range(RING):
        value = turn[pl.ds(strip, LANES, RING), :].T
        for at in range(3):
            inp[at, strip, pl.ds(OFF, own), :] = value[at * own:(at + 1) * own]
        inp[3, strip, pl.ds(OFF, own), :] = value[2 * own:3 * own] + value[3 * own:]

    far = REACH - own

    def move(at, row, row_there, rows, peer):
        return pltpu.make_async_remote_copy(
            inp.at[:, :, pl.ds(OFF + row, rows), :],
            inp.at[:, :, pl.ds(OFF + row_there, rows), :],
            send_sem.at[at], recv_sem.at[at],
            device_id={"space": peer}, device_id_type=MESH)

    down = [
        move(0, own - far, -far, far, after),
        move(1, 0, -own, own - far, after),
        move(2, -far, -own - far, far, after),
    ]
    up = [
        move(3, 0, own, far, before),
        move(4, far, own + far, own - far, before),
        move(5, own, 2 * own, far, before),
    ]
    down[0].start()
    down[1].start()
    pl.semaphore_wait(ready, 1)
    up[0].start()
    up[1].start()
    down[0].wait_recv()
    down[2].start()
    up[0].wait_recv()
    up[2].start()

    start = Field(inp, OFF)
    rates = Field(inp, OFF)

    def take(radius):
        at, _ = room(radius)
        return Field(fields.pop(0), at)

    first = [take(FULL[1][0]) for _ in range(2)]
    partials = [None] + [take(radii[0]) for radii in FULL[1:]]
    plan = []
    for radii in FULL:
        plan.append([{
            "force": take(radius) if radii is not FULL[0] else None,
            "work": [take(radius - at) for at in range(3)],
            "node": take(radius - 3)} for radius in radii])

    def react(u, v, feed, both):
        cubic = u * v * v
        return feed * (1.0 - u) - cubic, cubic - both * v

    def laps(node, row, rows):
        u, near_u = node.around(0, row, rows)
        v, near_v = node.around(1, row, rows)
        return (u, v), (near_u - 4.0 * u, 0.5 * near_v - 2.0 * v)

    def first_forcing(row, rows):
        feed, both = rates.load(2, row, rows), rates.load(3, row, rows)
        state, lap = laps(start, row, rows)
        rea = react(*state, feed, both)
        for field in range(2):
            total = lap[field] + rea[field]
            first[0].store(field, row, rows, (9.0 / 24.0) * total - rea[field])
            first[1].store(field, row, rows, (1.0 / 24.0) * total)

    def forcing(level_num, row, rows):
        feed, both = rates.load(2, row, rows), rates.load(3, row, rows)
        lap_of, rea_of = [], []
        for at in range(STEPS - 1):
            state, lap = laps(plan[level_num - 1][at]["node"], row, rows)
            lap_of.append(lap)
            rea_of.append(react(*state, feed, both))
        force = [step["force"] for step in plan[level_num]]
        for field in range(2):
            lap = [None] + [value[field] for value in lap_of]
            rea = [None] + [value[field] for value in rea_of]
            full = [None] + [a + b for a, b in zip(lap[1:], rea[1:])]
            nine = first[0].load(field, row, rows)
            one = first[1].load(field, row, rows)
            third = (1.0 / 24.0) * full[3]
            second = (5.0 / 24.0) * full[2]
            force[0].store(field, row, rows, (
                (nine - lap[1]) + (19.0 / 24.0) * full[1] - second + third))
            force[1].store(field, row, rows, (
                (13.0 / 24.0) * (full[1] + full[2]) - (one + third) - (lap[2] + rea[1])))
            force[2].store(field, row, rows, (
                (one - (lap[3] + rea[2])) - (5.0 / 24.0) * full[1]
                + (19.0 / 24.0) * full[2] + (9.0 / 24.0) * full[3]))
            partials[level_num].store(field, row, rows, (
                (1.0 / 24.0) * full[1] - second + (19.0 / 24.0) * full[3] - rea[3]))

    def finish(level_num, row, rows):
        feed, both = rates.load(2, row, rows), rates.load(3, row, rows)
        state, lap = laps(plan[level_num - 1][STEPS - 1]["node"], row, rows)
        rea = react(*state, feed, both)
        for field in range(2):
            plan[level_num][STEPS - 1]["force"].store(field, row, rows, (
                partials[level_num].load(field, row, rows)
                + ((9.0 / 24.0) * rea[field] - (15.0 / 24.0) * lap[field])))

    def source(state, force, dest, row, rows):
        feed, both = rates.load(2, row, rows), rates.load(3, row, rows)
        u, v = state.load(0, row, rows), state.load(1, row, rows)
        rea_u, rea_v = react(u, v, feed, both)
        u = u + rea_u
        v = v + rea_v
        if force is not None:
            u = u + force.load(0, row, rows)
            v = v + force.load(1, row, rows)
        dest.store(0, row, rows, 0.2 * u)
        dest.store(1, row, rows, (1.0 / 3.0) * v)

    def sweep(old, base, new, scales, row, rows):
        for field, scale in enumerate(scales):
            _, total = old.around(field, row, rows)
            if scale != 1.0:
                total = scale * total
            new.store(field, row, rows, base.load(field, row, rows) + total)

    def spans(flip, second, full, known):
        low, high = (-full, min(known, own + full)) if second else (known, own + full)
        if flip:
            low, high = own - high, own - low
        return [(low, high, not flip)]

    def run_level(flip, second, level_num):
        steps = plan[level_num]
        extents = list(zip(FULL[level_num], KNOWN[level_num]))
        if level_num == 1:
            over_rows(spans(flip, second, *extents[0]), 8, first_forcing)
        if level_num:
            over_rows(spans(flip, second, *extents[0]), 8, lambda row, rows: forcing(level_num, row, rows))
            over_rows(spans(flip, second, *extents[3]), 8, lambda row, rows: finish(level_num, row, rows))
        for step_num, step in enumerate(steps):
            state = start if step_num == 0 else steps[step_num - 1]["node"]
            work, (full, known) = step["work"], extents[step_num]
            over_rows(spans(flip, second, full, known), CHUNK,
                      lambda row, rows: source(state, step["force"], work[0], row, rows))
            for sweep_num in range(3):
                new = work[sweep_num + 1] if sweep_num < 2 else step["node"]
                scales = (0.2, 1.0 / 6.0) if sweep_num else (1.0, 0.5)
                over_rows(spans(flip, second, full - sweep_num - 1, known + sweep_num + 1), CHUNK,
                          lambda row, rows: sweep(work[sweep_num], work[0], new, scales, row, rows))

    def handles(level_num):
        place = out.at[0, :, :, pl.ds(pl.multiple_of(level * cols, LANES), cols)]
        mine = pltpu.make_async_copy(fin.at[level_num], place, put_sem.at[level_num])
        theirs = pltpu.make_async_remote_copy(
            fin.at[level_num], place, put_sem.at[level_num], got_sem.at[level],
            device_id={"level": level_num}, device_id_type=MESH)
        return mine, theirs

    def put(level_num):
        node = plan[level_num][STEPS - 1]["node"]
        for strip in range(RING):
            pair = [node.ref[field, strip, pl.ds(node.at, own), :] for field in range(2)]
            turn_out[pl.ds(strip, LANES, RING), :] = jnp.concatenate(pair, 0).T
        for tile in range(TILES):
            value = turn_out[pl.ds(tile * LANES, LANES), :].T
            for field in range(2):
                fin[level_num, field, :, pl.ds(tile * LANES, LANES)] = (
                    value[field * own:(field + 1) * own])
        mine, theirs = handles(level_num)

        @pl.when(level == level_num)
        def _():
            mine.start()

        @pl.when(level != level_num)
        def _():
            theirs.start()

    def window(flip):
        for second in (False, True):
            for copy in down[1:] if second != flip else up[1:]:
                copy.wait_recv()
            for level_num in range(LEVELS):
                run_level(flip, second, level_num)
                if second:
                    put(level_num)

    first_of_run = lax.rem(space, RUN) == 0

    @pl.when(first_of_run)
    def _():
        window(False)

    @pl.when(jnp.logical_not(first_of_run))
    def _():
        window(True)

    for copy in down + up:
        copy.wait_send()
    for level_num in range(LEVELS):
        mine, theirs = handles(level_num)

        @pl.when(level == level_num)
        def _():
            mine.wait()

        @pl.when(level != level_num)
        def _():
            theirs.wait_send()

    for step in range(1, LEVELS):
        source_level = lax.rem(level + step, LEVELS)
        place = out.at[0, :, :, pl.ds(pl.multiple_of(source_level * cols, LANES), cols)]
        pltpu.make_async_remote_copy(
            fin.at[0], place, put_sem.at[0], got_sem.at[source_level],
            device_id={"level": source_level}, device_id_type=MESH).wait_recv()


def body(u_init, v_init, feed_rate, kill_rate):
    own, width = u_init.shape
    dma = pltpu.SemaphoreType.DMA

    def pair(radius):
        return pltpu.VMEM((2, RING, room(radius)[1], LANES), jnp.float32)

    fields = [pair(FULL[1][0])] * 2 + [pair(radii[0]) for radii in FULL[1:]]
    for radii in FULL:
        for radius in radii:
            if radii is not FULL[0]:
                fields.append(pair(radius))
            fields += [pair(radius - at) for at in range(4)]
    return pl.pallas_call(
        lambda *refs: kernel(own, *refs),
        out_shape=pltpu.VMEM((1, 2, own, width), jnp.float32),
        in_specs=[pl.BlockSpec(memory_space=pltpu.HBM)] * 4,
        out_specs=pl.BlockSpec(memory_space=pl.ANY),
        scratch_shapes=[
            pltpu.VMEM((4, RING, OFF + own + OFF + 8, LANES), jnp.float32),
            pltpu.VMEM((TILES + 2, 4 * own, LANES), jnp.float32),
            pltpu.VMEM((RING * LANES, 4 * own), jnp.float32),
            pltpu.VMEM((LEVELS, 2, own, TILES * LANES), jnp.float32),
            pltpu.VMEM((RING * LANES, 2 * own), jnp.float32),
        ] + fields + [
            dma((TILES + 2, 4)), dma((6,)), dma((6,)), dma((LEVELS,)), dma((LEVELS,)),
            pltpu.SemaphoreType.REGULAR,
        ],
        compiler_params=pltpu.CompilerParams(
            collective_id=0, has_side_effects=True, vmem_limit_bytes=48 * 1024 * 1024),
        name="window",
    )(*[pltpu.with_memory_space_constraint(x, pltpu.HBM) for x in (u_init, v_init, feed_rate, kill_rate)])


def solution(mesh):
    return jax.shard_map(
        body,
        mesh=mesh,
        in_specs=(P("space", None),) * 4,
        out_specs=P("level", None, "space", None),
        check_vma=False,
    )
```

time: 48 us -> 34.8 us (0.72)
  Pallas kernels: 43.1 us -> 33.9 us
  local copies, waits for them, and re-layouts: 4.59 us -> 0.8 us
    pallas_call x1, Pallas kernels: 43.1 us -> 33.9 us  [body(): pl.pallas_call(lambda *refs: kernel(own, *refs), out_shape=pltpu.VMEM((1,...]
    unnamed x9 -> x1, local copies, waits for them, and re-layouts: 4.59 us -> 0.8 us
where the time goes in v1:
time: 34.8 us; the launch traced here: 34.7 us
  Pallas kernels  33.9 us (97%)
  local copies, waits for them, and re-layouts  0.8 us (2%)
    pallas_call x1, Pallas kernels, body(): pl.pallas_call(lambda *refs: kernel(own, *refs), out_shape=pltpu.VMEM((1,...  33.9 us
    unnamed x1, local copies, waits for them, and re-layouts  0.8 us

profile of v1, /device:TPU:3, one launch (start us, length us, event | category | flops | bytes accessed | tf_op | source)
XLA Modules:
  0.0 34.7 jit_solution(316381684081224602)
XLA Ops:
  0.0 33.9 %window.1 = f32[1,2,32,2048]{3,2,1,0:T(8,128)S(1)} custom-call(f32[32,2048]{1,0:T(8,128)} %refs_0_.1, f32[32,2048]{1,0:T(8,128)} %refs_1_.1, f32[32,2048]{1,0:T(8,128)} %refs_2_.1, f32[32,2048]{1,0:T(8,128)} %refs_3_.1), custom_call_target="tpu_custom_call" | custom-call | tf_op jit(solution)/shard_map/window/pallas_call | solution.py:327
  33.9 0.8 %copy.6 = f32[1,2,32,2048]{3,2,1,0:T(8,128)} copy(f32[1,2,32,2048]{3,2,1,0:T(8,128)S(1)} %window.1) | data formatting | bytes 1048576

commit v2 on v1

--- a/solution.py
+++ b/solution.py
@@ -12,11 +12,13 @@
 RING = TILES + 1
 OFF = 48
 REACH = 42
+REACH_NEAR = 26
 CHUNK = 16
 RUN = 4
 MESH = pl.DeviceIdType.MESH
 
 FULL = [[42, 39, 36, 15], [32, 29, 26, 11], [22, 19, 16, 7], [12, 9, 6, 3]]
+NEAR = [[26, 23, 20, 15], [16, 13, 10, 7], [6, 3, 0, -3], [-4, -7, -10, -13]]
 KNOWN = [[10 * level + 3 * step + 6 for step in range(STEPS)] for level in range(LEVELS)]
 
 
@@ -26,20 +28,29 @@
 
 
 class Field:
-    def __init__(self, ref, at):
-        self.ref, self.at = ref, at
-
-    def load(self, field, row, rows):
-        return self.ref[field, :, pl.ds(row + self.at, rows), :]
+    def __init__(self, ref, at, side=0):
+        self.ref, self.at, self.side = ref, at, side
+
+    def load(self, field, row, rows, side=0):
+        strips = pl.ds(self.side - side, RING + 2 * side)
+        return self.ref[field, strips, pl.ds(row + self.at, rows), :]
 
     def store(self, field, row, rows, value):
+        if self.side > (value.shape[0] - RING) // 2:
+            value = jnp.concatenate([
+                pltpu.roll(value[RING - self.side:], 1, 2), value,
+                pltpu.roll(value[:self.side], LANES - 1, 2)], 0)
         self.ref[field, :, pl.ds(row + self.at, rows), :] = value
 
-    def around(self, field, row, rows):
-        mid = self.load(field, row, rows)
-        left = jnp.concatenate([pltpu.roll(mid[RING - 1:], 1, 2), mid[:RING - 1]], 0)
-        right = jnp.concatenate([mid[1:], pltpu.roll(mid[:1], LANES - 1, 2)], 0)
-        vertical = self.load(field, row - 1, rows) + self.load(field, row + 1, rows)
+    def around(self, field, row, rows, side=0):
+        if self.side > side:
+            wide = self.load(field, row, rows, side + 1)
+            mid, left, right = wide[1:-1], wide[:-2], wide[2:]
+        else:
+            mid = self.load(field, row, rows)
+            left = jnp.concatenate([pltpu.roll(mid[RING - 1:], 1, 2), mid[:RING - 1]], 0)
+            right = jnp.concatenate([mid[1:], pltpu.roll(mid[:1], LANES - 1, 2)], 0)
+        vertical = self.load(field, row - 1, rows, side) + self.load(field, row + 1, rows, side)
         return mid, (left + right) + vertical
 
 
@@ -112,30 +123,32 @@
 
     down = [
         move(0, own - far, -far, far, after),
-        move(1, 0, -own, own - far, after),
-        move(2, -far, -own - far, far, after),
+        move(1, own - REACH_NEAR, -REACH_NEAR, REACH_NEAR - far, after),
+        move(2, 0, -own, own - REACH_NEAR, after),
+        move(3, -far, -own - far, far, after),
     ]
     up = [
-        move(3, 0, own, far, before),
-        move(4, far, own + far, own - far, before),
-        move(5, own, 2 * own, far, before),
+        move(4, 0, own, far, before),
+        move(5, far, own + far, REACH_NEAR - far, before),
+        move(6, REACH_NEAR, own + REACH_NEAR, own - REACH_NEAR, before),
+        move(7, own, 2 * own, far, before),
     ]
-    down[0].start()
-    down[1].start()
+    for copy in down[:3]:
+        copy.start()
     pl.semaphore_wait(ready, 1)
-    up[0].start()
-    up[1].start()
+    for copy in up[:3]:
+        copy.start()
     down[0].wait_recv()
-    down[2].start()
+    down[3].start()
     up[0].wait_recv()
-    up[2].start()
+    up[3].start()
 
     start = Field(inp, OFF)
     rates = Field(inp, OFF)
 
-    def take(radius):
+    def take(radius, side=0):
         at, _ = room(radius)
-        return Field(fields.pop(0), at)
+        return Field(fields.pop(0), at, side)
 
     first = [take(FULL[1][0]) for _ in range(2)]
     partials = [None] + [take(radii[0]) for radii in FULL[1:]]
@@ -143,7 +156,7 @@
     for radii in FULL:
         plan.append([{
             "force": take(radius) if radii is not FULL[0] else None,
-            "work": [take(radius - at) for at in range(3)],
+            "work": [take(radius - at, 2 - at) for at in range(3)],
             "node": take(radius - 3)} for radius in radii])
 
     def react(u, v, feed, both):
@@ -213,74 +226,91 @@
 
     def sweep(old, base, new, scales, row, rows):
         for field, scale in enumerate(scales):
-            _, total = old.around(field, row, rows)
+            _, total = old.around(field, row, rows, new.side)
             if scale != 1.0:
                 total = scale * total
-            new.store(field, row, rows, base.load(field, row, rows) + total)
-
-    def spans(flip, second, full, known):
-        low, high = (-full, min(known, own + full)) if second else (known, own + full)
+            new.store(field, row, rows, base.load(field, row, rows, new.side) + total)
+
+    def spans(flip, stage, full, near, known):
+        known = min(known, own + full)
+        low, high = {"below": (known, own + full), "near": (-near, known), "far": (-full, -near)}[stage]
         if flip:
             low, high = own - high, own - low
         return [(low, high, not flip)]
 
-    def run_level(flip, second, level_num):
+    def run_level(flip, stage, level_num):
         steps = plan[level_num]
-        extents = list(zip(FULL[level_num], KNOWN[level_num]))
+        extents = list(zip(FULL[level_num], NEAR[level_num], KNOWN[level_num]))
         if level_num == 1:
-            over_rows(spans(flip, second, *extents[0]), 8, first_forcing)
+            over_rows(spans(flip, stage, *extents[0]), 8, first_forcing)
         if level_num:
-            over_rows(spans(flip, second, *extents[0]), 8, lambda row, rows: forcing(level_num, row, rows))
-            over_rows(spans(flip, second, *extents[3]), 8, lambda row, rows: finish(level_num, row, rows))
+            over_rows(spans(flip, stage, *extents[0]), 8, lambda row, rows: forcing(level_num, row, rows))
+            over_rows(spans(flip, stage, *extents[3]), 8, lambda row, rows: finish(level_num, row, rows))
         for step_num, step in enumerate(steps):
             state = start if step_num == 0 else steps[step_num - 1]["node"]
-            work, (full, known) = step["work"], extents[step_num]
-            over_rows(spans(flip, second, full, known), CHUNK,
+            work, (full, near, known) = step["work"], extents[step_num]
+            over_rows(spans(flip, stage, full, near, known), CHUNK,
                       lambda row, rows: source(state, step["force"], work[0], row, rows))
             for sweep_num in range(3):
                 new = work[sweep_num + 1] if sweep_num < 2 else step["node"]
                 scales = (0.2, 1.0 / 6.0) if sweep_num else (1.0, 0.5)
-                over_rows(spans(flip, second, full - sweep_num - 1, known + sweep_num + 1), CHUNK,
+                over_rows(spans(
+                    flip, stage, full - sweep_num - 1, near - sweep_num - 1, known + sweep_num + 1), CHUNK,
                           lambda row, rows: sweep(work[sweep_num], work[0], new, scales, row, rows))
 
-    def handles(level_num):
-        place = out.at[0, :, :, pl.ds(pl.multiple_of(level * cols, LANES), cols)]
-        mine = pltpu.make_async_copy(fin.at[level_num], place, put_sem.at[level_num])
+    part = own // 2
+
+    def handles(level_num, half):
+        rows = pl.ds(half * part, part)
+        place = out.at[0, :, rows, pl.ds(pl.multiple_of(level * cols, LANES), cols)]
+        mine = pltpu.make_async_copy(fin.at[level_num, :, rows], place, put_sem.at[level_num, half])
         theirs = pltpu.make_async_remote_copy(
-            fin.at[level_num], place, put_sem.at[level_num], got_sem.at[level],
+            fin.at[level_num, :, rows], place, put_sem.at[level_num, half], got_sem.at[level, half],
             device_id={"level": level_num}, device_id_type=MESH)
         return mine, theirs
 
-    def put(level_num):
+    def put(level_num, halves):
         node = plan[level_num][STEPS - 1]["node"]
+        first_row, count = halves[0] * part, len(halves) * part
+        lanes = pl.ds(0, 2 * count)
         for strip in range(RING):
-            pair = [node.ref[field, strip, pl.ds(node.at, own), :] for field in range(2)]
-            turn_out[pl.ds(strip, LANES, RING), :] = jnp.concatenate(pair, 0).T
+            pair = [node.ref[field, strip, pl.ds(node.at + first_row, count), :] for field in range(2)]
+            turn_out[pl.ds(strip, LANES, RING), lanes] = jnp.concatenate(pair, 0).T
         for tile in range(TILES):
-            value = turn_out[pl.ds(tile * LANES, LANES), :].T
+            value = turn_out[pl.ds(tile * LANES, LANES), lanes].T
             for field in range(2):
-                fin[level_num, field, :, pl.ds(tile * LANES, LANES)] = (
-                    value[field * own:(field + 1) * own])
-        mine, theirs = handles(level_num)
+                fin[level_num, field, pl.ds(first_row, count), pl.ds(tile * LANES, LANES)] = (
+                    value[field * count:(field + 1) * count])
 
         @pl.when(level == level_num)
         def _():
-            mine.start()
+            for half in halves:
+                handles(level_num, half)[0].start()
 
         @pl.when(level != level_num)
         def _():
-            theirs.start()
+            for half in halves:
+                handles(level_num, half)[1].start()
 
     def window(flip):
-        for second in (False, True):
-            for copy in down[1:] if second != flip else up[1:]:
-                copy.wait_recv()
-            for level_num in range(LEVELS):
-                run_level(flip, second, level_num)
-                if second:
-                    put(level_num)
-
-    first_of_run = lax.rem(space, RUN) == 0
+        early, late = (down, up) if flip else (up, down)
+        known_first, known_last = (0, 1) if flip else (1, 0)
+        for copy in early[1:]:
+            copy.wait_recv()
+        for level_num in range(LEVELS):
+            run_level(flip, "below", level_num)
+        late[1].wait_recv()
+        for level_num in range(LEVELS):
+            run_level(flip, "near", level_num)
+            put(level_num, (0, 1) if level_num < 2 else (known_first,))
+        late[2].wait_recv()
+        late[3].wait_recv()
+        for level_num in range(LEVELS):
+            run_level(flip, "far", level_num)
+            if level_num >= 2:
+                put(level_num, (known_last,))
+
+    first_of_run = lax.rem(space, RUN) < RUN // 2
 
     @pl.when(first_of_run)
     def _():
@@ -293,37 +323,39 @@
     for copy in down + up:
         copy.wait_send()
     for level_num in range(LEVELS):
-        mine, theirs = handles(level_num)
-
         @pl.when(level == level_num)
         def _():
-            mine.wait()
+            for half in range(2):
+                handles(level_num, half)[0].wait()
 
         @pl.when(level != level_num)
         def _():
-            theirs.wait_send()
+            for half in range(2):
+                handles(level_num, half)[1].wait_send()
 
     for step in range(1, LEVELS):
         source_level = lax.rem(level + step, LEVELS)
-        place = out.at[0, :, :, pl.ds(pl.multiple_of(source_level * cols, LANES), cols)]
-        pltpu.make_async_remote_copy(
-            fin.at[0], place, put_sem.at[0], got_sem.at[source_level],
-            device_id={"level": source_level}, device_id_type=MESH).wait_recv()
+        for half in range(2):
+            rows = pl.ds(half * part, part)
+            place = out.at[0, :, rows, pl.ds(pl.multiple_of(source_level * cols, LANES), cols)]
+            pltpu.make_async_remote_copy(
+                fin.at[0, :, rows], place, put_sem.at[0, half], got_sem.at[source_level, half],
+                device_id={"level": source_level}, device_id_type=MESH).wait_recv()
 
 
 def body(u_init, v_init, feed_rate, kill_rate):
     own, width = u_init.shape
     dma = pltpu.SemaphoreType.DMA
 
-    def pair(radius):
-        return pltpu.VMEM((2, RING, room(radius)[1], LANES), jnp.float32)
+    def pair(radius, side=0):
+        return pltpu.VMEM((2, RING + 2 * side, room(radius)[1], LANES), jnp.float32)
 
     fields = [pair(FULL[1][0])] * 2 + [pair(radii[0]) for radii in FULL[1:]]
     for radii in FULL:
         for radius in radii:
             if radii is not FULL[0]:
                 fields.append(pair(radius))
-            fields += [pair(radius - at) for at in range(4)]
+            fields += [pair(radius - at, max(2 - at, 0)) for at in range(4)]
     return pl.pallas_call(
         lambda *refs: kernel(own, *refs),
         out_shape=pltpu.VMEM((1, 2, own, width), jnp.float32),
@@ -336,11 +368,11 @@
             pltpu.VMEM((LEVELS, 2, own, TILES * LANES), jnp.float32),
             pltpu.VMEM((RING * LANES, 2 * own), jnp.float32),
         ] + fields + [
-            dma((TILES + 2, 4)), dma((6,)), dma((6,)), dma((LEVELS,)), dma((LEVELS,)),
+            dma((TILES + 2, 4)), dma((8,)), dma((8,)), dma((LEVELS, 2)), dma((LEVELS, 2)),
             pltpu.SemaphoreType.REGULAR,
         ],
         compiler_params=pltpu.CompilerParams(
-            collective_id=0, has_side_effects=True, vmem_limit_bytes=48 * 1024 * 1024),
+            collective_id=0, has_side_effects=True, vmem_limit_bytes=56 * 1024 * 1024),
         name="window",
     )(*[pltpu.with_memory_space_constraint(x, pltpu.HBM) for x in (u_init, v_init, feed_rate, kill_rate)])
 

time: 34.8 us -> 32.2 us (0.925)
  Pallas kernels: 33.9 us -> 31.3 us
    pallas_call x1, Pallas kernels: 33.9 us -> 31.3 us  [body(): pl.pallas_call(lambda *refs: kernel(own, *refs), out_shape=pltpu.VMEM((1,...]
where the time goes in v2:
time: 32.2 us; the launch traced here: 32.1 us
  Pallas kernels  31.3 us (97%)
  local copies, waits for them, and re-layouts  0.8 us (2%)
    pallas_call x1, Pallas kernels, body(): pl.pallas_call(lambda *refs: kernel(own, *refs), out_shape=pltpu.VMEM((1,...  31.3 us
    unnamed x1, local copies, waits for them, and re-layouts  0.8 us

profile of v2, /device:TPU:3, one launch (start us, length us, event | category | flops | bytes accessed | tf_op | source)
XLA Modules:
  0.0 32.1 jit_solution(11733577038198080833)
XLA Ops:
  0.0 31.3 %window.1 = f32[1,2,32,2048]{3,2,1,0:T(8,128)S(1)} custom-call(f32[32,2048]{1,0:T(8,128)} %refs_0_.1, f32[32,2048]{1,0:T(8,128)} %refs_1_.1, f32[32,2048]{1,0:T(8,128)} %refs_2_.1, f32[32,2048]{1,0:T(8,128)} %refs_3_.1), custom_call_target="tpu_custom_call" | custom-call | tf_op jit(solution)/shard_map/window/pallas_call | solution.py:359
  31.3 0.8 %copy.6 = f32[1,2,32,2048]{3,2,1,0:T(8,128)} copy(f32[1,2,32,2048]{3,2,1,0:T(8,128)S(1)} %window.1) | data formatting | bytes 1048576

commit v3 on v2

--- a/solution.py
+++ b/solution.py
@@ -14,6 +14,7 @@
 REACH = 42
 REACH_NEAR = 26
 CHUNK = 16
+PARTS = 4
 RUN = 4
 MESH = pl.DeviceIdType.MESH
 
@@ -138,10 +139,6 @@
     pl.semaphore_wait(ready, 1)
     for copy in up[:3]:
         copy.start()
-    down[0].wait_recv()
-    down[3].start()
-    up[0].wait_recv()
-    up[3].start()
 
     start = Field(inp, OFF)
     rates = Field(inp, OFF)
@@ -231,34 +228,40 @@
                 total = scale * total
             new.store(field, row, rows, base.load(field, row, rows, new.side) + total)
 
-    def spans(flip, stage, full, near, known):
+    def spans(stage, full, near, known):
+        name, flip = stage
         known = min(known, own + full)
-        low, high = {"below": (known, own + full), "near": (-near, known), "far": (-full, -near)}[stage]
+        rows = {
+            "half": [(known, own + near, True)],
+            "below": [(max(known, own + near), own + full, False)],
+            "near": [(-near, known, True)],
+            "far": [(-full, -near, True)],
+        }[name]
         if flip:
-            low, high = own - high, own - low
-        return [(low, high, not flip)]
-
-    def run_level(flip, stage, level_num):
+            rows = [(own - high, own - low, not upward) for low, high, upward in rows]
+        return rows
+
+    def run_level(stage, level_num):
         steps = plan[level_num]
         extents = list(zip(FULL[level_num], NEAR[level_num], KNOWN[level_num]))
         if level_num == 1:
-            over_rows(spans(flip, stage, *extents[0]), 8, first_forcing)
+            over_rows(spans(stage, *extents[0]), 8, first_forcing)
         if level_num:
-            over_rows(spans(flip, stage, *extents[0]), 8, lambda row, rows: forcing(level_num, row, rows))
-            over_rows(spans(flip, stage, *extents[3]), 8, lambda row, rows: finish(level_num, row, rows))
+            over_rows(spans(stage, *extents[0]), 8, lambda row, rows: forcing(level_num, row, rows))
+            over_rows(spans(stage, *extents[3]), 8, lambda row, rows: finish(level_num, row, rows))
         for step_num, step in enumerate(steps):
             state = start if step_num == 0 else steps[step_num - 1]["node"]
             work, (full, near, known) = step["work"], extents[step_num]
-            over_rows(spans(flip, stage, full, near, known), CHUNK,
+            over_rows(spans(stage, full, near, known), CHUNK,
                       lambda row, rows: source(state, step["force"], work[0], row, rows))
             for sweep_num in range(3):
                 new = work[sweep_num + 1] if sweep_num < 2 else step["node"]
                 scales = (0.2, 1.0 / 6.0) if sweep_num else (1.0, 0.5)
                 over_rows(spans(
-                    flip, stage, full - sweep_num - 1, near - sweep_num - 1, known + sweep_num + 1), CHUNK,
+                    stage, full - sweep_num - 1, near - sweep_num - 1, known + sweep_num + 1), CHUNK,
                           lambda row, rows: sweep(work[sweep_num], work[0], new, scales, row, rows))
 
-    part = own // 2
+    part = own // PARTS
 
     def handles(level_num, half):
         rows = pl.ds(half * part, part)
@@ -271,16 +274,19 @@
 
     def put(level_num, halves):
         node = plan[level_num][STEPS - 1]["node"]
-        first_row, count = halves[0] * part, len(halves) * part
+        count = len(halves) * part
         lanes = pl.ds(0, 2 * count)
         for strip in range(RING):
-            pair = [node.ref[field, strip, pl.ds(node.at + first_row, count), :] for field in range(2)]
-            turn_out[pl.ds(strip, LANES, RING), lanes] = jnp.concatenate(pair, 0).T
+            pieces = [node.ref[field, strip, pl.ds(node.at + half * part, part), :]
+                      for field in range(2) for half in halves]
+            turn_out[pl.ds(strip, LANES, RING), lanes] = jnp.concatenate(pieces, 0).T
         for tile in range(TILES):
             value = turn_out[pl.ds(tile * LANES, LANES), lanes].T
             for field in range(2):
-                fin[level_num, field, pl.ds(first_row, count), pl.ds(tile * LANES, LANES)] = (
-                    value[field * count:(field + 1) * count])
+                for at, half in enumerate(halves):
+                    row = field * count + at * part
+                    fin[level_num, field, pl.ds(half * part, part), pl.ds(tile * LANES, LANES)] = (
+                        value[row:row + part])
 
         @pl.when(level == level_num)
         def _():
@@ -292,50 +298,54 @@
             for half in halves:
                 handles(level_num, half)[1].start()
 
-    def window(flip):
+    every = tuple(range(PARTS))
+
+    def one_side(flip):
         early, late = (down, up) if flip else (up, down)
-        known_first, known_last = (0, 1) if flip else (1, 0)
-        for copy in early[1:]:
+        early[0].wait_recv()
+        early[3].start()
+        early[1].wait_recv()
+        for level_num in range(LEVELS):
+            run_level(("half", flip), level_num)
+        late[0].wait_recv()
+        late[3].start()
+        for copy in early[2:]:
             copy.wait_recv()
         for level_num in range(LEVELS):
-            run_level(flip, "below", level_num)
+            run_level(("below", flip), level_num)
         late[1].wait_recv()
         for level_num in range(LEVELS):
-            run_level(flip, "near", level_num)
-            put(level_num, (0, 1) if level_num < 2 else (known_first,))
+            run_level(("near", flip), level_num)
+            pieces = (every, every, (1, 2, 3), (2, 3))[level_num]
+            put(level_num, tuple(sorted(PARTS - 1 - piece for piece in pieces)) if flip else pieces)
         late[2].wait_recv()
         late[3].wait_recv()
         for level_num in range(LEVELS):
-            run_level(flip, "far", level_num)
+            run_level(("far", flip), level_num)
             if level_num >= 2:
-                put(level_num, (known_last,))
-
-    first_of_run = lax.rem(space, RUN) < RUN // 2
-
-    @pl.when(first_of_run)
-    def _():
-        window(False)
-
-    @pl.when(jnp.logical_not(first_of_run))
-    def _():
-        window(True)
+                pieces = ((0,), (0, 1))[level_num - 2]
+                put(level_num, tuple(sorted(PARTS - 1 - piece for piece in pieces)) if flip else pieces)
+
+    first_half = lax.rem(space, RUN) < RUN // 2
+    pl.when(first_half)(lambda: one_side(False))
+    pl.when(jnp.logical_not(first_half))(lambda: one_side(True))
 
     for copy in down + up:
         copy.wait_send()
     for level_num in range(LEVELS):
         @pl.when(level == level_num)
         def _():
-            for half in range(2):
+            for half in range(PARTS):
                 handles(level_num, half)[0].wait()
 
         @pl.when(level != level_num)
         def _():
-            for half in range(2):
+            for half in range(PARTS):
                 handles(level_num, half)[1].wait_send()
 
     for step in range(1, LEVELS):
         source_level = lax.rem(level + step, LEVELS)
-        for half in range(2):
+        for half in range(PARTS):
             rows = pl.ds(half * part, part)
             place = out.at[0, :, rows, pl.ds(pl.multiple_of(source_level * cols, LANES), cols)]
             pltpu.make_async_remote_copy(
@@ -368,7 +378,7 @@
             pltpu.VMEM((LEVELS, 2, own, TILES * LANES), jnp.float32),
             pltpu.VMEM((RING * LANES, 2 * own), jnp.float32),
         ] + fields + [
-            dma((TILES + 2, 4)), dma((8,)), dma((8,)), dma((LEVELS, 2)), dma((LEVELS, 2)),
+            dma((TILES + 2, 4)), dma((8,)), dma((8,)), dma((LEVELS, PARTS)), dma((LEVELS, PARTS)),
             pltpu.SemaphoreType.REGULAR,
         ],
         compiler_params=pltpu.CompilerParams(

time: 32.2 us -> 33.2 us (1.031)
  the two profiles are of different devices: /device:TPU:3 before, /device:TPU:39 now
where the time goes in v3:
time: 33.2 us; the launch traced here: 33 us
  Pallas kernels  32.2 us (97%)
  local copies, waits for them, and re-layouts  0.8 us (2%)
    pallas_call x1, Pallas kernels, body(): pl.pallas_call(lambda *refs: kernel(own, *refs), out_shape=pltpu.VMEM((1,...  32.2 us
    unnamed x1, local copies, waits for them, and re-layouts  0.8 us

profile of v3, /device:TPU:39, one launch (start us, length us, event | category | flops | bytes accessed | tf_op | source)
XLA Modules:
  0.0 33.0 jit_solution(15964507195088749690)
XLA Ops:
  0.0 32.2 %window.1 = f32[1,2,32,2048]{3,2,1,0:T(8,128)S(1)} custom-call(f32[32,2048]{1,0:T(8,128)} %refs_0_.1, f32[32,2048]{1,0:T(8,128)} %refs_1_.1, f32[32,2048]{1,0:T(8,128)} %refs_2_.1, f32[32,2048]{1,0:T(8,128)} %refs_3_.1), custom_call_target="tpu_custom_call" | custom-call | tf_op jit(solution)/shard_map/window/pallas_call | solution.py:369
  32.2 0.8 %copy.6 = f32[1,2,32,2048]{3,2,1,0:T(8,128)} copy(f32[1,2,32,2048]{3,2,1,0:T(8,128)S(1)} %window.1) | data formatting | bytes 1048576
